TPU v7x, 32 devices: a whole 2x2x4 slice. The times are simulated.
32 devices in a mesh: parts: 2 (over y), sub: 4 (over z), row: 2 (over x), col: 2 (over core).
Axes of the slice: x: 2, y: 2, z: 4, core: 2. Of those that a mesh axis runs over, the one named last changes fastest.
Arguments:
- loads: float32 [8, 32, 1024], P(('parts', 'sub'), 'col'), parts along dimension 0, may hold values from -6 to 6
- weights: float32 [8, 1024], P(('parts', 'sub')), parts along dimension 0, may hold values from 0.25 to 4
- dual_ops: bfloat16 [8, 2048, 2048], P(('parts', 'sub'), 'row'), parts along dimension 0, as said below
- corner_maps: bfloat16 [8, 24, 2048], P(('parts', 'sub'), None, 'row'), parts along dimension 0, may hold values from -0.25 to 0.25
- coarse_inverse: float32 [96, 48], P('parts'), parts along dimension 0, as said below
- corner_ids: int32 [8, 24], P('parts'), parts along dimension 0, may hold values from 0 to 47, as said below
- iface_sizes: int32 [8], P('parts'), parts along dimension 0, may hold values from 512 to 1024, as said below
- left_partner: int32 [8, 1024], P(('parts', 'sub')), parts along dimension 0, may hold values from 0 to 1023, as said below
- right_partner: int32 [8, 1024], P(('parts', 'sub')), parts along dimension 0, may hold values from 0 to 1023, as said below
Outputs:
- solution: float32 [8, 32, 1024], P(('parts', 'sub'), 'col'), parts along dimension 0
- residual: float32 [8, 32, 1024], P(('parts', 'sub'), 'col'), parts along dimension 0
There are 2 independent parts, one for each index of `parts`. A program takes and returns all parts, laid end to end along the dimension named above; each array names one. Nothing has to cross between parts.
Inputs may be any that keep to these rules, and one draw needn't show every extreme that they name: Global indices 24/2 * s to 24/2 * s + 24/2 - 1 are the corners of the interface between s and s+1; the first half of subdomain s's corner_ids is a permutation of those of interface s-1, the second half a permutation of those of interface s. `left_partner`: each row s is a permutation that maps the slots below iface_sizes[s-1] onto slots below it. `right_partner`: each row s is a permutation that maps the slots below iface_sizes[s] onto slots below it, and is the inverse of left_partner[s+1]. `dual_ops`: symmetric positive definite. `coarse_inverse`: symmetric positive definite. For each s < 2, one of iface_sizes[s] and iface_sizes[s + 2] is 896 or more and the other 640 or less.
All inputs are finite; a program needn't handle non-finite values.
Results may differ from a plain program's by a relative error of at most 0.015.
Values may be sent and summed in bfloat16 or wider, within the bound.
A program may use at most 64 MiB of HBM per device.

v0:
```python
import jax
import jax.numpy as jnp
from jax import lax
from jax.sharding import PartitionSpec as P

TILE = 128
ITERS = 2


def shifted(value, axis, steps):
    count = lax.axis_size(axis)
    pairs = [(source, (source + steps) % count) for source in range(count)]
    return lax.ppermute(value, axis, pairs)


def inner(first, second, half):
    return jnp.sum(first[:, :half] * second[:, :half], axis=1)


def paired_totals(residual, precond, image, half):
    return lax.psum((inner(residual, precond, half), inner(precond, image, half)), "sub")


def tile_products(vector, rows_op, first_tile, last_tile, output):

    def one_tile(tile_at, acc):
        piece = lax.dynamic_slice_in_dim(rows_op, tile_at * TILE, TILE, 0)
        product = lax.dot_general(
            vector, piece, (((1,), (1,)), ((), ())), preferred_element_type=jnp.float32
        )
        return lax.dynamic_update_slice_in_dim(acc, product, tile_at * TILE, 1)

    return lax.fori_loop(first_tile, last_tile, one_tile, output)


def live_tiles(size_before, size_after, block_start, block, half):
    left_live = jnp.clip(size_before - block_start, 0, block)
    right_live = jnp.clip(size_after - (block_start - half), 0, block)
    live_cols = jnp.where(block_start < half, left_live, right_live)
    return (live_cols + TILE - 1) // TILE


def per_device(
    loads,
    weights,
    dual_ops,
    corner_maps,
    coarse_inverse,
    corner_ids,
    iface_sizes,
    left_partner,
    right_partner,
):
    half = loads.shape[2]
    block = dual_ops.shape[1]
    width = coarse_inverse.shape[0]
    subdomain = lax.axis_index("sub")
    count = lax.axis_size("sub")
    row_index = lax.axis_index("row")
    left_map = left_partner[0]
    right_map = right_partner[0]
    slots = jnp.arange(half, dtype=jnp.int32)
    size_before = iface_sizes[(subdomain + count - 1) % count]
    size_after = iface_sizes[subdomain]
    live_left = (slots < size_before).astype(jnp.float32)
    live_right = (right_map < size_after).astype(jnp.float32)
    columns = jnp.arange(width, dtype=jnp.int32)
    own_hot = (corner_ids[subdomain][:, None] == columns[None, :]).astype(jnp.float32)
    operator = dual_ops[0]
    coupling = corner_maps[0]
    block_start = row_index * block
    own_tiles = live_tiles(size_before, size_after, block_start, block, half)

    def apply_operator(vec):
        halfway = vec.astype(jnp.bfloat16)
        empty = jnp.zeros((halfway.shape[0], block), jnp.float32)
        local = tile_products(halfway, operator, jnp.int32(0), own_tiles, empty)
        own_slots = lax.dynamic_slice_in_dim(halfway, row_index * block, block, 1)
        corner = lax.dot_general(
            own_slots, coupling, (((1,), (1,)), ((), ())), preferred_element_type=jnp.float32
        )
        scattered = jnp.dot(corner, own_hot, precision=lax.Precision.HIGHEST)
        coarse = lax.psum(scattered, ("sub", "row"))
        solved = jnp.dot(coarse, coarse_inverse, precision=lax.Precision.HIGHEST)
        back = lax.dot_general(
            solved, own_hot, (((1,), (1,)), ((), ())), precision=lax.Precision.HIGHEST
        ).astype(jnp.bfloat16)
        united = local + jnp.dot(back, coupling, preferred_element_type=jnp.float32)
        whole = lax.all_gather(united.astype(jnp.bfloat16), "row", axis=1, tiled=True).astype(
            united.dtype
        )
        lower = whole[:, :half]
        upper = whole[:, half:]
        arrived_left = shifted(upper.astype(jnp.bfloat16), "sub", 1).astype(upper.dtype)
        arrived_right = shifted(lower.astype(jnp.bfloat16), "sub", -1).astype(lower.dtype)
        result_left = (lower + jnp.take(arrived_left, left_map, axis=1)) * live_left
        result_right = (upper + jnp.take(arrived_right, right_map, axis=1)) * live_right
        return jnp.concatenate([result_left, result_right], axis=1)

    received = (
        shifted(loads[0].astype(jnp.bfloat16), "sub", -1).astype(jnp.float32),
        shifted(weights.astype(jnp.bfloat16), "sub", -1).astype(weights.dtype),
    )
    right_load = jnp.take(received[0], right_map, axis=1) * live_right
    right_weight = jnp.take(received[1], right_map, axis=1)
    residual = jnp.concatenate([loads[0] * live_left, right_load], axis=1)
    scaling = jnp.concatenate([weights, right_weight], axis=1)
    solution = jnp.zeros_like(residual)
    precond = scaling * residual
    image = apply_operator(precond)
    gamma, delta = paired_totals(residual, precond, image, half)
    alpha = gamma / delta
    direction = precond
    along = image
    for step in range(ITERS):
        solution = solution + alpha[:, None] * direction
        residual = residual - alpha[:, None] * along
        if step + 1 < ITERS:
            precond = scaling * residual
            image = apply_operator(precond)
            gamma_next, delta = paired_totals(residual, precond, image, half)
            ratio = gamma_next / gamma
            alpha = gamma_next / (delta - ratio * gamma_next / alpha)
            direction = precond + ratio[:, None] * direction
            along = image + ratio[:, None] * along
            gamma = gamma_next
    return (solution[:, :half][None], residual[:, :half][None])


def solution(mesh):
    placed = (
        P(("parts", "sub"), "col", None),
        P(("parts", "sub"), None),
        P(("parts", "sub"), "row", None),
        P(("parts", "sub"), None, "row"),
        P("parts", None),
        P("parts", None),
        P("parts"),
        P(("parts", "sub"), None),
        P(("parts", "sub"), None),
    )
    return jax.shard_map(
        per_device,
        mesh=mesh,
        in_specs=placed,
        out_specs=(P(("parts", "sub"), "col", None), P(("parts", "sub"), "col", None)),
        check_vma=False,
    )
```

profile of v0, /device:TPU:0, one launch (start us, length us, event | category | flops | bytes accessed | tf_op | source)
XLA Modules:
  0.0 136.2 jit_solution(17909804324471528583)
XLA Ops:
  0.7 0.9 bitcast_convert_fusion
  1.5 5.1 %collective-permute-start.1 = (bf16[16,1024]{1,0:T(8,128)(2,1)S(1)}, bf16[16,1024]{1,0:T(8,128)(2,1)S(1)}, u32[]{:S(2)}, u32[]{:S(2)}) collective-permute-start(bf16[16,1024]{1,0:T(8,128)(2,1)S(1)} %bitcast_convert_fusion), channel_id=1, source_target_pairs={{0,12},{4,0},{8,4},{12,8},{1,13},{5,1},{9,5},{13,9},{2,14},{6,2},{... | collective-permute-start | bytes 98312 | tf_op jit(solution)/shard_map/ppermute | solution.py:13
  6.6 0.7 convert_element_type.71
  7.3 0.4 collective-permute-start
  7.8 0.7 compare_select_fusion
  8.4 0.7 fusion.36
  9.1 1.3 fusion.49
  10.5 1.3 fusion.35
  11.8 1.3 compare_convert_fusion
  13.1 0.8 bitcast_multiply_fusion.1
  14.0 0.7 fusion.40
  14.7 0.7 fusion.37
  16.7 4.5 %gather_fusion = f32[1024]{0:T(1024)S(1)} fusion(f32[1024]{0:T(1024)S(1)} %bitcast.80, s32[1024]{0:T(1024)S(1)} %broadcast_clamp_fusion), kind=kCustom, calls=%fused_computation.5 | custom fusion | bytes 12288 | tf_op jit(solution)/shard_map/jit(_take)/gather | solution.py:105
  21.4 0.1 copy.21
  21.5 2.8 %gather_fusion.1 = f32[1024,16]{1,0:T(8,128)S(1)} fusion(f32[16,1024]{0,1:T(8,128)S(1)} %copy.21, s32[1024]{0:T(1024)S(1)} %fusion.36), kind=kCustom, calls=%fused_computation.clone | custom fusion | bytes 135168 | tf_op jit(solution)/shard_map/jit(_take)/gather | solution.py:104
  24.3 0.2 copy.22
  24.5 10.4 %while.20 = (s32[]{:T(128)}, f32[16,1024]{1,0:T(8,128)S(1)}, s32[]{:T(128)}, bf16[1024,2048]{1,0:T(8,128)(2,1)}, bf16[16,2048]{1,0:T(8,128)(2,1)S(1)}, /*index=5*/s32[]{:T(128)}, s32[]{:T(128)}, s32[]{:T(128)}, s32[]{:T(128)}) while((s32[]{:T(128)}, f32[16,1024]{1,0:T(8,128)S(1)}, s32[]{:T(128)}, bf16[1024,2048]{1,0:T(8,128)(2,1)}, ...), condition=%wide.region_3.5_spmd, body=%wide.region_2.4_spmd.sunk | while | flops 8388614 | bytes 599179 | solution.py:33
  24.6 1.3 fusion.72
  25.9 1.3 fusion.72
  27.1 1.3 fusion.72
  28.4 1.3 fusion.72
  29.7 1.3 fusion.72
  31.0 1.3 fusion.72
  32.3 1.3 fusion.72
  33.6 1.3 fusion.72
  34.9 0.1 fusion.25
  35.1 0.2 fusion.30
  35.3 18.8 %psum.43 = f32[16,48]{1,0:T(8,128)S(1)} all-reduce(f32[16,48]{1,0:T(8,128)S(1)} %fusion.30), channel_id=1, replica_groups=mesh['parts'=2,'sub'=4,'row'=2,'col'=2] {'sub','row'}, use_global_device_ids=true, to_apply=%region_4.6 | all-reduce | flops 768 | bytes 6144 | tf_op jit(solution)/shard_map/psum | solution.py:83
  54.2 0.2 convolution_convert_fusion.1
  54.4 0.1 fusion.6
  54.5 4.6 %all_gather.6 = bf16[16,2048]{1,0:T(8,128)(2,1)S(1)} all-gather(bf16[16,1024]{1,0:T(8,128)(2,1)S(1)} %fusion.6), channel_id=1, replica_groups=mesh['parts'=2,'sub'=4,'row'=2,'col'=2] {'row'}, dimensions={1}, use_global_device_ids=true | all-gather | bytes 98304 | tf_op jit(solution)/shard_map/all_gather | solution.py:89
  59.1 3.8 %collective-permute-start.3 = (bf16[16,1024]{1,0:T(8,128)(2,1)S(1)}, bf16[16,1024]{1,0:T(8,128)(2,1)S(1)}, u32[]{:S(2)}, u32[]{:S(2)}) collective-permute-start(bf16[16,1024]{1,0:T(8,128)(2,1)S(1)} %get-tuple-element.103), channel_id=1, source_target_pairs={{0,12},{4,0},{8,4},{12,8},{1,13},{5,1},{9,5},{13,9},{2,14},{6,2},{... | collective-permute-start | bytes 98312 | tf_op jit(solution)/shard_map/ppermute | solution.py:13
  63.0 1.9 %collective-permute-done.2 = bf16[16,1024]{1,0:T(8,128)(2,1)S(1)} collective-permute-done((bf16[16,1024]{1,0:T(8,128)(2,1)S(1)}, bf16[16,1024]{1,0:T(8,128)(2,1)S(1)}, u32[]{:S(2)}, u32[]{:S(2)}) %collective-permute-start.2) | collective-permute-done | bytes 32800 | tf_op jit(solution)/shard_map/ppermute | solution.py:13
  64.9 2.8 %gather_fusion.2 = f32[1024,16]{1,0:T(8,128)S(1)} fusion(f32[16,1024]{0,1:T(8,128)S(1)} %copy.23, s32[1024]{0:T(1024)S(1)} %fusion.37), kind=kCustom, calls=%fused_computation.1.clone | custom fusion | bytes 135168 | tf_op jit(solution)/shard_map/jit(_take)/gather | solution.py:96
  67.8 0.2 copy.24
  67.9 0.1 copy.25
  68.1 2.8 %gather_fusion.3 = f32[1024,16]{1,0:T(8,128)S(1)} fusion(f32[16,1024]{0,1:T(8,128)S(1)} %copy.25, s32[1024]{0:T(1024)S(1)} %fusion.36), kind=kCustom, calls=%fused_computation.2.clone | custom fusion | bytes 135168 | tf_op jit(solution)/shard_map/jit(_take)/gather | solution.py:97
  70.9 0.2 copy.26
  71.1 0.1 multiply_reduce_fusion.2
  71.2 9.1 %all-reduce.1 = (f32[16]{0:T(128)S(1)}, f32[16]{0:T(128)S(1)}) all-reduce(f32[16]{0:T(128)S(1)} %get-tuple-element.64, f32[16]{0:T(128)S(1)} %get-tuple-element.63), channel_id=1, replica_groups=mesh['parts'=2,'sub'=4,'row'=2,'col'=2] {'sub'}, use_global_device_ids=true, to_apply=%region_1.3 | all-reduce | flops 32 | bytes 256 | tf_op jit(solution)/shard_map/psum | solution.py:21
  80.5 10.3 %while.21 = (s32[]{:T(128)}, f32[16,1024]{1,0:T(8,128)S(1)}, s32[]{:T(128)}, bf16[1024,2048]{1,0:T(8,128)(2,1)}, bf16[16,2048]{1,0:T(8,128)(2,1)S(1)}, /*index=5*/s32[]{:T(128)}, s32[]{:T(128)}, s32[]{:T(128)}, s32[]{:T(128)}) while((s32[]{:T(128)}, f32[16,1024]{1,0:T(8,128)S(1)}, s32[]{:T(128)}, bf16[1024,2048]{1,0:T(8,128)(2,1)}, ...), condition=%wide.region_10.12_spmd, body=%wide.region_9.11_spmd.sunk | while | flops 8388614 | bytes 599179 | solution.py:33
  80.5 1.3 fusion.75
  81.8 1.3 fusion.75
  83.1 1.3 fusion.75
  84.4 1.3 fusion.75
  85.7 1.3 fusion.75
  87.0 1.3 fusion.75
  88.3 1.3 fusion.75
  89.6 1.3 fusion.75
  90.9 0.2 fusion.29
  91.1 18.8 %psum.46 = f32[16,48]{1,0:T(8,128)S(1)} all-reduce(f32[16,48]{1,0:T(8,128)S(1)} %fusion.29), channel_id=1, replica_groups=mesh['parts'=2,'sub'=4,'row'=2,'col'=2] {'sub','row'}, use_global_device_ids=true, to_apply=%region_11.13 | all-reduce | flops 768 | bytes 6144 | tf_op jit(solution)/shard_map/psum | solution.py:83
  110.0 0.2 convolution_convert_fusion
  110.2 0.1 fusion.7
  110.3 4.6 %all_gather.7 = bf16[16,2048]{1,0:T(8,128)(2,1)S(1)} all-gather(bf16[16,1024]{1,0:T(8,128)(2,1)S(1)} %fusion.7), channel_id=1, replica_groups=mesh['parts'=2,'sub'=4,'row'=2,'col'=2] {'row'}, dimensions={1}, use_global_device_ids=true | all-gather | bytes 98304 | tf_op jit(solution)/shard_map/all_gather | solution.py:89
  114.9 2.0 %collective-permute-start.4 = (bf16[16,1024]{1,0:T(8,128)(2,1)S(1)}, bf16[16,1024]{1,0:T(8,128)(2,1)S(1)}, u32[]{:S(2)}, u32[]{:S(2)}) collective-permute-start(bf16[16,1024]{1,0:T(8,128)(2,1)S(1)} %get-tuple-element.101), channel_id=1, source_target_pairs={{0,4},{4,8},{8,12},{12,0},{1,5},{5,9},{9,13},{13,1},{2,6},{6,10},{... | collective-permute-start | bytes 98312 | tf_op jit(solution)/shard_map/ppermute | solution.py:13
  117.0 1.9 %collective-permute-done.5 = bf16[16,1024]{1,0:T(8,128)(2,1)S(1)} collective-permute-done((bf16[16,1024]{1,0:T(8,128)(2,1)S(1)}, bf16[16,1024]{1,0:T(8,128)(2,1)S(1)}, u32[]{:S(2)}, u32[]{:S(2)}) %collective-permute-start.5) | collective-permute-done | bytes 32800 | tf_op jit(solution)/shard_map/ppermute | solution.py:13
  119.0 2.8 %gather_fusion.5 = f32[1024,16]{1,0:T(8,128)S(1)} fusion(f32[16,1024]{0,1:T(8,128)S(1)} %copy.29, s32[1024]{0:T(1024)S(1)} %fusion.36), kind=kCustom, calls=%fused_computation.4.clone | custom fusion | bytes 135168 | tf_op jit(solution)/shard_map/jit(_take)/gather | solution.py:97
  121.8 0.2 copy.30
  122.0 0.1 copy.27
  122.1 2.8 %gather_fusion.4 = f32[1024,16]{1,0:T(8,128)S(1)} fusion(f32[16,1024]{0,1:T(8,128)S(1)} %copy.27, s32[1024]{0:T(1024)S(1)} %fusion.37), kind=kCustom, calls=%fused_computation.3.clone | custom fusion | bytes 135168 | tf_op jit(solution)/shard_map/jit(_take)/gather | solution.py:96
  124.9 0.2 copy.28
  125.1 0.1 multiply_reduce_fusion
  125.2 10.2 %all-reduce = (f32[16]{0:T(128)S(1)}, f32[16]{0:T(128)S(1)}) all-reduce(f32[16]{0:T(128)S(1)} %get-tuple-element.62, f32[16]{0:T(128)S(1)} %get-tuple-element.61), channel_id=1, replica_groups=mesh['parts'=2,'sub'=4,'row'=2,'col'=2] {'sub'}, use_global_device_ids=true, to_apply=%region_8.10 | all-reduce | flops 32 | bytes 256 | tf_op jit(solution)/shard_map/psum | solution.py:21
  135.4 0.7 fusion.16
  (39 shorter events, 1.0 us)
Async XLA Ops:
  0.6 34.3 %copy-start = (bf16[1,24,1024]{2,1,0:T(8,128)(2,1)S(1)}, bf16[1,24,1024]{2,1,0:T(8,128)(2,1)}, u32[]{:S(2)}) copy-start(bf16[1,24,1024]{2,1,0:T(8,128)(2,1)} %param.18) | copy-start | bytes 147460
  0.6 20.7 %copy-start.5 = (f32[1,1024]{1,0:T(1,128)S(1)}, f32[1,1024]{1,0:T(1,128)}, u32[]{:S(2)}) copy-start(f32[1,1024]{1,0:T(1,128)} %param.16) | copy-start | bytes 12292
  0.7 20.6 %copy-start.2 = (s32[1,1024]{1,0:T(1,128)S(1)}, s32[1,1024]{1,0:T(1,128)}, u32[]{:S(2)}) copy-start(s32[1,1024]{1,0:T(1,128)} %param.23) | copy-start | bytes 12292
  1.5 19.8 %collective-permute-start.1 = (bf16[16,1024]{1,0:T(8,128)(2,1)S(1)}, bf16[16,1024]{1,0:T(8,128)(2,1)S(1)}, u32[]{:S(2)}, u32[]{:S(2)}) collective-permute-start(bf16[16,1024]{1,0:T(8,128)(2,1)S(1)} %bitcast_convert_fusion), channel_id=1, source_target_pairs={{0,12},{4,0},{8,4},{12,8},{1,13},{5,1},{9,5},{13,9},{2,14},{6,2},{... | collective-permute-start | bytes 98312 | tf_op jit(solution)/shard_map/ppermute | solution.py:13
  7.3 9.4 %collective-permute-start = (bf16[1,1024]{1,0:T(2,128)(2,1)S(1)}, bf16[1,1024]{1,0:T(2,128)(2,1)S(1)}, u32[]{:S(2)}, u32[]{:S(2)}) collective-permute-start(bf16[1,1024]{1,0:T(2,128)(2,1)S(1)} %convert_element_type.71), channel_id=1, source_target_pairs={{0,12},{4,0},{8,4},{12,8},{1,13},{5,1},{9,5},{13,9},{2,14},{6,2},{... | collective-permute-start | bytes 6152 | tf_op jit(solution)/shard_map/ppermute | solution.py:13
  16.7 37.3 %copy-start.3 = (f32[48,48]{1,0:T(8,128)S(1)}, f32[48,48]{1,0:T(8,128)}, u32[]{:S(2)}) copy-start(f32[48,48]{1,0:T(8,128)} %param.19) | copy-start | bytes 27652
  16.7 46.2 %copy-start.4 = (s32[1,1024]{1,0:T(1,128)S(1)}, s32[1,1024]{1,0:T(1,128)}, u32[]{:S(2)}) copy-start(s32[1,1024]{1,0:T(1,128)} %param.22) | copy-start | bytes 12292
  24.5 46.6 %copy-start.1 = (f32[1,16,1024]{2,1,0:T(8,128)S(1)}, f32[1,16,1024]{2,1,0:T(8,128)}, u32[]{:S(2)}) copy-start(f32[1,16,1024]{2,1,0:T(8,128)} %param.15) | copy-start | bytes 196612
  59.1 5.7 %collective-permute-start.2 = (bf16[16,1024]{1,0:T(8,128)(2,1)S(1)}, bf16[16,1024]{1,0:T(8,128)(2,1)S(1)}, u32[]{:S(2)}, u32[]{:S(2)}) collective-permute-start(bf16[16,1024]{1,0:T(8,128)(2,1)S(1)} %get-tuple-element.102), channel_id=1, source_target_pairs={{0,4},{4,8},{8,12},{12,0},{1,5},{5,9},{9,13},{13,1},{2,6},{6,10},{... | collective-permute-start | bytes 98312 | tf_op jit(solution)/shard_map/ppermute | solution.py:13
  59.1 8.8 %collective-permute-start.3 = (bf16[16,1024]{1,0:T(8,128)(2,1)S(1)}, bf16[16,1024]{1,0:T(8,128)(2,1)S(1)}, u32[]{:S(2)}, u32[]{:S(2)}) collective-permute-start(bf16[16,1024]{1,0:T(8,128)(2,1)S(1)} %get-tuple-element.103), channel_id=1, source_target_pairs={{0,12},{4,0},{8,4},{12,8},{1,13},{5,1},{9,5},{13,9},{2,14},{6,2},{... | collective-permute-start | bytes 98312 | tf_op jit(solution)/shard_map/ppermute | solution.py:13
  114.9 3.9 %collective-permute-start.5 = (bf16[16,1024]{1,0:T(8,128)(2,1)S(1)}, bf16[16,1024]{1,0:T(8,128)(2,1)S(1)}, u32[]{:S(2)}, u32[]{:S(2)}) collective-permute-start(bf16[16,1024]{1,0:T(8,128)(2,1)S(1)} %get-tuple-element.100), channel_id=1, source_target_pairs={{0,12},{4,0},{8,4},{12,8},{1,13},{5,1},{9,5},{13,9},{2,14},{6,2},{... | collective-permute-start | bytes 98312 | tf_op jit(solution)/shard_map/ppermute | solution.py:13
  114.9 7.0 %collective-permute-start.4 = (bf16[16,1024]{1,0:T(8,128)(2,1)S(1)}, bf16[16,1024]{1,0:T(8,128)(2,1)S(1)}, u32[]{:S(2)}, u32[]{:S(2)}) collective-permute-start(bf16[16,1024]{1,0:T(8,128)(2,1)S(1)} %get-tuple-element.101), channel_id=1, source_target_pairs={{0,4},{4,8},{8,12},{12,0},{1,5},{5,9},{9,13},{13,1},{2,6},{6,10},{... | collective-permute-start | bytes 98312 | tf_op jit(solution)/shard_map/ppermute | solution.py:13
where the time goes:
time: 137 us; the launch traced here: 136 us
  blocking collectives  65.9 us (48%)
  matrix products  22.3 us (16%)
  local copies, waits for them, and re-layouts  22.1 us (16%)
  starting transfers between devices  11.4 us (8%)
  other arithmetic  8.41 us (6%)
  waiting for transfers between devices  3.74 us (3%)
  between operations  2.25 us (2%)
    psum x2, blocking collectives, apply_operator(): coarse = lax.psum(scattered, ('sub', 'row'))  37.5 us
    dot_general x16, matrix products, one_tile(): lax.dot_general(vector, piece, (((1,), (1,)), ((), ())), preferred_elemen...  20.7 us
    psum x2, blocking collectives, paired_totals(): lax.psum((inner(residual, precond, half), inner(precond, image, half)), '...  19.2 us
    ppermute x6, starting transfers between devices, shifted(): return lax.ppermute(value, axis, pairs)  11.4 us
    all_gather x2, blocking collectives, apply_operator(): lax.all_gather(united.astype(jnp.bfloat16), 'row', axis=1, tiled=True)  9.15 us
    gather x4, local copies, waits for them, and re-layouts, apply_operator(): result_left = (lower + jnp.take(arrived_left, left_map, axis=1)) * live_left  5.95 us
    gather x4, local copies, waits for them, and re-layouts, apply_operator(): jnp.take(arrived_right, right_map, axis=1)  5.95 us
    gather x1, local copies, waits for them, and re-layouts, per_device(): right_weight = jnp.take(received[1], right_map, axis=1)  4.53 us
  transfers between devices with their start and end apart: 6, of which 2 were waited for; matrix products, arithmetic and copies ran while one was open for 14% of the time, Pallas kernels for 0%

commit v1 on v0

v1 whole, which is shorter than its diff:
```python
import functools

import jax
import jax.numpy as jnp
from jax import lax
from jax.experimental import pallas as pl
from jax.experimental.pallas import tpu as pltpu
from jax.sharding import PartitionSpec as P

MESH = pl.DeviceIdType.MESH
CHUNK = 256
BF = jnp.bfloat16
F32 = jnp.float32


def each(count, body):
    if count <= 8:
        for at in range(count):
            body(at)
    else:
        lax.fori_loop(0, count, lambda at, _: (body(at), 0)[1], 0)


def dot_nt(a, b):
    return lax.dot_general(a, b, (((1,), (1,)), ((), ())), preferred_element_type=F32)


def dot_nn(a, b):
    return lax.dot_general(a, b, (((1,), (0,)), ((), ())), preferred_element_type=F32)


def kernel(
    S, R, loads, weights, op, cm, cinv, ids, sizes, lmap, rmap, sol, res,
    loads_v, w_v, op_v, cv, cinv_p, ids_v, lmap_v, rmap_v,
    zsend, zrecv, wrecv, cmo, cmn, mo, mn, pl_m, pr_m, zs,
    own, nbr, pk,
    in_sem, op_sem, z_sem, cmo_ssem, cmo_rsem, cmn_ssem, cmn_rsem,
    own_ssem, own_rsem, nbr_ssem, nbr_rsem, pk_ssem, pk_rsem,
):
    s = lax.axis_index("sub")
    r = lax.axis_index("row")
    G = S * R
    me = s * R + r
    C, H = loads_v.shape
    B = op_v.shape[0]
    NC = cv.shape[0]
    W = cinv_p.shape[0]
    half_r = R // 2
    nxt = lax.rem(s + 1, S)
    prv = lax.rem(s + S - 1, S)
    side = r // half_r
    toward = lax.rem(s + S - 1 + 2 * side, S)

    ins = [
        pltpu.make_async_copy(src, dst, in_sem.at[i])
        for i, (src, dst) in enumerate([
            (loads.at[0], loads_v), (weights, w_v), (rmap, rmap_v), (lmap, lmap_v),
            (ids, ids_v), (cinv, cv), (cm.at[0], cmo.at[r]),
        ])
    ]
    for copy in ins:
        copy.start()
    chunk = min(CHUNK, B)
    ops = [
        pltpu.make_async_copy(
            op.at[0, pl.ds(c * chunk, chunk), :], op_v.at[pl.ds(c * chunk, chunk), :], op_sem.at[c]
        )
        for c in range(B // chunk)
    ]
    for copy in ops:
        copy.start()

    barrier = pltpu.get_barrier_semaphore()

    def peer(k):
        g = lax.rem(me + k + 1, G)
        return g, {"sub": g // R, "row": lax.rem(g, R)}

    def greet(k):
        _, who = peer(k)
        pl.semaphore_signal(barrier, inc=1, device_id=who, device_id_type=MESH)

    each(G - 1, greet)

    size_before = sizes[prv]
    size_after = sizes[s]
    lanes = lax.broadcasted_iota(jnp.int32, (1, H), 1)
    live_l = (lanes < size_before).astype(F32)
    ins[0].wait()
    ins[1].wait()
    w_l = w_v[...]
    r0 = loads_v[...] * live_l
    z0 = w_l * r0
    zsend[...] = z0.astype(BF)

    pl.semaphore_wait(barrier, G - 1)

    def remote(src, dst, ssem, rsem, who):
        return pltpu.make_async_remote_copy(
            src_ref=src, dst_ref=dst, send_sem=ssem, recv_sem=rsem, device_id=who, device_id_type=MESH
        )

    z_copy = remote(zsend, zrecv, z_sem.at[0], z_sem.at[1], {"sub": prv})
    w_copy = remote(weights, wrecv, z_sem.at[2], z_sem.at[3], {"sub": prv})
    z_copy.start()
    w_copy.start()

    def to_row(src, dst, ssem, rsem, k):
        q = lax.rem(r + k, R)
        return remote(src, dst.at[r], ssem.at[k], rsem.at[r], {"row": q})

    def to_side(src, dst, ssem, rsem, k):
        q = lax.rem(r + k, R)
        return remote(src, dst.at[r], ssem.at[k], rsem.at[r], {"sub": toward, "row": q})

    def wait_slot(dst, ssem, rsem, q):
        remote(dst.at[q], dst.at[q], ssem.at[0], rsem.at[q], {"sub": nxt}).wait_recv()

    cm_sends = [to_row(cm.at[0], cmo, cmo_ssem, cmo_rsem, k) for k in range(1, R)]
    cm_sends += [to_side(cm.at[0], cmn, cmn_ssem, cmn_rsem, k) for k in range(R)]
    for copy in cm_sends:
        copy.start()

    ins[2].wait()
    ins[3].wait()
    right_map = rmap_v[...]
    left_map = lmap_v[...]
    live_r = (right_map < size_after).astype(F32)

    def hot(target, the_map):
        step = 128
        for c in range(H // step):
            rows = lax.broadcasted_iota(jnp.int32, (step, H), 0) + c * step
            target[pl.ds(c * step, step), :] = (rows == the_map).astype(F32).astype(BF)

    hot(pr_m, right_map)
    hot(pl_m, left_map)
    ins[4].wait()
    ins[5].wait()
    cinv_p[...] = jnp.zeros_like(cinv_p)
    cinv_p[0:NC, 0:NC] = cv[...]

    def hot_ids(t):
        row = ids_v[pl.ds(t, 1), :]
        rows = lax.broadcasted_iota(jnp.int32, (W, row.shape[1]), 0)
        return (rows == row).astype(F32).astype(BF)

    hot_own = hot_ids(s)
    ins[6].wait()
    mo[r] = dot_nn(hot_own, cmo[r]).astype(BF)

    z_copy.wait_recv()
    w_copy.wait_recv()
    w_in = wrecv[...]
    w_hi = w_in.astype(BF)
    w_lo = (w_in - w_hi.astype(F32)).astype(BF)
    pad = lax.broadcasted_iota(jnp.int32, (16, H), 0)
    w_rows = jnp.where(pad == 0, w_hi.astype(F32), jnp.where(pad == 1, w_lo.astype(F32), 0.0))
    gathered = dot_nn(jnp.concatenate([zrecv[...], w_rows.astype(BF)], axis=0), pr_m[...])
    z0_r = gathered[:C]
    w_r = gathered[C : C + 1] + gathered[C + 1 : C + 2]

    col = lax.broadcasted_iota(jnp.int32, (C, W), 1)

    def pick(value, lane):
        return jnp.sum(jnp.where(col == lane, value, 0.0), axis=1, keepdims=True)

    def product(step, z_left, z_right, r_left):
        full = jnp.concatenate([z_left.astype(BF), z_right.astype(BF)], axis=1)
        for q in range(R):
            half = z_left if q < half_r else z_right
            at = (q % half_r) * B
            zs[q] = half[:, at : at + B]
        parts = []
        for c in range(B // chunk):
            if step == 0:
                ops[c].wait()
            parts.append(dot_nt(full, op_v[c * chunk : (c + 1) * chunk, :]))
        local = jnp.concatenate(parts, axis=1)
        own[step, r] = local.astype(BF)
        mine = own.at[step, r]
        sends = [
            to_side(mine, nbr.at[step], nbr_ssem.at[step], nbr_rsem.at[step], k) for k in range(R)
        ]
        sends += [
            to_row(mine, own.at[step], own_ssem.at[step], own_rsem.at[step], k) for k in range(1, R)
        ]
        for copy in sends:
            copy.start()
        block = zs[r]
        delta = jnp.sum(block * local, axis=1, keepdims=True)
        gamma = jnp.sum(r_left * z_left, axis=1, keepdims=True)
        gamma = jnp.where(r == 0, gamma, 0.0)
        corner = dot_nt(block.astype(BF), mo[r])
        packet = corner + jnp.where(col == NC, gamma, 0.0) + jnp.where(col == NC + 1, delta, 0.0)
        pk[step, me] = packet

        def spread(k):
            _, who = peer(k)
            remote(
                pk.at[step, me], pk.at[step, me], pk_ssem.at[step, k], pk_rsem.at[step, me], who
            ).start()

        each(G - 1, spread)
        return sends

    def collect(step, need_right):
        def arrive(k):
            g, who = peer(k)
            remote(
                pk.at[step, g], pk.at[step, g], pk_ssem.at[step, 0], pk_rsem.at[step, g], who
            ).wait_recv()

        each(G - 1, arrive)
        if G <= 8:
            total = pk[step, 0]
            for g in range(1, G):
                total = total + pk[step, g]
        else:
            total = lax.fori_loop(
                0, G, lambda g, acc: acc + pk[step, g], jnp.zeros((C, W), F32)
            )
        solved = lax.dot_general(
            total, cinv_p[...], (((1,), (0,)), ((), ())),
            precision=lax.Precision.HIGHEST, preferred_element_type=F32,
        )
        back = solved.astype(BF)
        gamma = pick(total, NC)
        delta = pick(total, NC + 1) + jnp.sum(total * back.astype(F32), axis=1, keepdims=True)
        for k in range(1, R):
            wait_slot(own.at[step], own_ssem.at[step], own_rsem.at[step], lax.rem(r + k, R))
        for q in range(R):
            wait_slot(nbr.at[step], nbr_ssem.at[step], nbr_rsem.at[step], q)

        def joined(store, maps, first, last):
            return jnp.concatenate(
                [store[step, q].astype(F32) + dot_nn(back, maps[q]) for q in range(first, last)], axis=1
            )

        from_prev = joined(nbr, mn, half_r, R).astype(BF)
        w_left = (joined(own, mo, 0, half_r) + dot_nn(from_prev, pl_m[...])) * live_l
        w_right = None
        if need_right:
            from_next = joined(nbr, mn, 0, half_r).astype(BF)
            w_right = (joined(own, mo, half_r, R) + dot_nn(from_next, pr_m[...])) * live_r
        return gamma, delta, w_left, w_right

    sends0 = product(0, z0, z0_r, r0)

    for k in range(1, R):
        q = lax.rem(r + k, R)
        wait_slot(cmo, cmo_ssem, cmo_rsem, q)
        mo[q] = dot_nn(hot_own, cmo[q]).astype(BF)
    hot_next = hot_ids(nxt)
    hot_prev = hot_ids(prv)
    for q in range(R):
        wait_slot(cmn, cmn_ssem, cmn_rsem, q)
        mn[q] = dot_nn(hot_next if q < half_r else hot_prev, cmn[q]).astype(BF)

    gamma0, delta0, wl0, wr0 = collect(0, True)
    alpha0 = gamma0 / delta0
    r1 = r0 - alpha0 * wl0
    z1 = w_l * r1
    z1_r = z0_r - alpha0 * (w_r * wr0)
    sends1 = product(1, z1, z1_r, r1)
    gamma1, delta1, wl1, _ = collect(1, False)
    beta = gamma1 / gamma0
    alpha1 = gamma1 / (delta1 - beta * gamma1 / alpha0)
    sol[...] = alpha0 * z0 + alpha1 * (z1 + beta * z0)
    res[...] = r1 - alpha1 * (wl1 + beta * wl0)

    z_copy.wait_send()
    w_copy.wait_send()
    for copy in cm_sends + sends0 + sends1:
        copy.wait_send()
    for step in range(2):

        def drain(k):
            _, who = peer(k)
            remote(
                pk.at[step, me], pk.at[step, me], pk_ssem.at[step, k], pk_rsem.at[step, me], who
            ).wait_send()

        each(G - 1, drain)


def per_device(S, R, loads, weights, dual_ops, corner_maps, coarse_inverse, corner_ids,
               iface_sizes, left_partner, right_partner):
    _, C, H = loads.shape
    _, B, full = dual_ops.shape
    J = corner_maps.shape[1]
    NC = coarse_inverse.shape[0]
    W = (NC + 2 + 127) // 128 * 128
    G = S * R
    DMA = pltpu.SemaphoreType.DMA
    anywhere = pl.BlockSpec(memory_space=pl.ANY)
    vmem = pl.BlockSpec(memory_space=pltpu.VMEM)
    out = jax.ShapeDtypeStruct((C, H), F32)
    sol, res = pl.pallas_call(
        functools.partial(kernel, S, R),
        out_shape=(out, out),
        in_specs=[anywhere] * 6 + [pl.BlockSpec(memory_space=pltpu.SMEM)] + [anywhere] * 2,
        out_specs=(vmem, vmem),
        scratch_shapes=[
            pltpu.VMEM((C, H), F32), pltpu.VMEM((1, H), F32), pltpu.VMEM((B, full), BF),
            pltpu.VMEM((NC, NC), F32), pltpu.VMEM((W, W), F32), pltpu.VMEM(corner_ids.shape, jnp.int32),
            pltpu.VMEM((1, H), jnp.int32), pltpu.VMEM((1, H), jnp.int32),
            pltpu.VMEM((C, H), BF), pltpu.VMEM((C, H), BF), pltpu.VMEM((1, H), F32),
            pltpu.VMEM((R, J, B), BF), pltpu.VMEM((R, J, B), BF),
            pltpu.VMEM((R, W, B), BF), pltpu.VMEM((R, W, B), BF),
            pltpu.VMEM((H, H), BF), pltpu.VMEM((H, H), BF), pltpu.VMEM((R, C, B), F32),
            pltpu.VMEM((2, R, C, B), BF), pltpu.VMEM((2, R, C, B), BF), pltpu.VMEM((2, G, C, W), F32),
            DMA((7,)), DMA((B // min(CHUNK, B),)), DMA((4,)), DMA((R,)), DMA((R,)), DMA((R,)), DMA((R,)),
            DMA((2, R)), DMA((2, R)), DMA((2, R)), DMA((2, R)), DMA((2, G)), DMA((2, G)),
        ],
        compiler_params=pltpu.CompilerParams(
            collective_id=0, has_side_effects=True, vmem_limit_bytes=48 * 1024 * 1024
        ),
    )(loads, weights, dual_ops, corner_maps, coarse_inverse, corner_ids, iface_sizes,
      left_partner, right_partner)
    return sol[None], res[None]


def solution(mesh):
    placed = (
        P(("parts", "sub"), "col", None),
        P(("parts", "sub"), None),
        P(("parts", "sub"), "row", None),
        P(("parts", "sub"), None, "row"),
        P("parts", None),
        P("parts", None),
        P("parts"),
        P(("parts", "sub"), None),
        P(("parts", "sub"), None),
    )
    return jax.shard_map(
        functools.partial(per_device, mesh.shape["sub"], mesh.shape["row"]),
        mesh=mesh,
        in_specs=placed,
        out_specs=(P(("parts", "sub"), "col", None), P(("parts", "sub"), "col", None)),
        check_vma=False,
    )
```

time: 137 us -> 37.5 us (0.27)
  blocking collectives: 65.9 us -> 0 us
  Pallas kernels: 0 us -> 27.1 us
  matrix products: 22.3 us -> 0 us
  local copies, waits for them, and re-layouts: 22.1 us -> 9.21 us
  starting transfers between devices: 11.4 us -> 0 us
  other arithmetic: 8.41 us -> 0 us
  waiting for transfers between devices: 3.74 us -> 0 us
  between operations: 2.25 us -> 0.66 us
    psum x4 -> x0, blocking collectives: 56.8 us -> none  [the longest x2 37.5 us: apply_operator(): coarse = lax.psum(scattered, ('sub', 'row'))]
    pallas_call x0 -> x1, Pallas kernels: none -> 27.1 us  [per_device(): pl.pallas_call(functools.partial(kernel, S, R), out_shape=(out, out), in_...]
    dot_general x26 -> x0, matrix products: 22.3 us -> none  [the longest x16 20.7 us: one_tile(): lax.dot_general(vector, piece, (((1,), (1,)), ((), ())), preferred_elemen...]
    gather x11 -> x0, local copies, waits for them, and re-layouts: 19.4 us -> none  [the longest x4 5.95 us: apply_operator(): result_left = (lower + jnp.take(arrived_left, left_map, axis=1)) * live_left]
    ppermute x6 -> x0, starting transfers between devices: 11.4 us -> none  [shifted(): return lax.ppermute(value, axis, pairs)]
    unnamed x12 -> x20, local copies, waits for them, and re-layouts: 0.04 us -> 9.21 us
    all_gather x2 -> x0, blocking collectives: 9.15 us -> none  [apply_operator(): lax.all_gather(united.astype(jnp.bfloat16), 'row', axis=1, tiled=True)]
    ppermute x6 -> x0, waiting for transfers between devices: 3.74 us -> none  [shifted(): return lax.ppermute(value, axis, pairs)]
  transfers between devices with their start and end apart: 6 -> 0, of which waited for: 2 -> 0; matrix products, arithmetic and copies ran while one was open for 14% -> 0% of each run, Pallas kernels for 0% -> 0%
where the time goes in v1:
time: 37.5 us; the launch traced here: 37 us
  Pallas kernels  27.1 us (72%)
  local copies, waits for them, and re-layouts  9.21 us (25%)
  between operations  0.66 us (2%)
    pallas_call x1, Pallas kernels, per_device(): pl.pallas_call(functools.partial(kernel, S, R), out_shape=(out, out), in_...  27.1 us
    unnamed x20, local copies, waits for them, and re-layouts  9.21 us

profile of v1, /device:TPU:0, one launch (start us, length us, event | category | flops | bytes accessed | tf_op | source)
XLA Modules:
  0.0 37.0 jit_solution(13330648287423019495)
XLA Ops:
  0.6 0.0 copy-start
  0.6 2.2 %copy-done = bf16[1,1024,2048]{2,1,0:T(8,128)(2,1)S(1)} copy-done((bf16[1,1024,2048]{2,1,0:T(8,128)(2,1)S(1)}, bf16[1,1024,2048]{2,1,0:T(8,128)(2,1)}, u32[]{:S(2)}) %copy-start) | copy-done | bytes 4194328
  2.8 0.0 copy-start.1
  2.8 0.8 %copy-done.1 = f32[1,16,1024]{2,1,0:T(8,128)S(1)} copy-done((f32[1,16,1024]{2,1,0:T(8,128)S(1)}, f32[1,16,1024]{2,1,0:T(8,128)}, u32[]{:S(2)}) %copy-start.1) | copy-done | bytes 65560
  3.7 0.0 copy-start.2
  3.7 0.8 %copy-done.2 = bf16[1,24,1024]{2,1,0:T(8,128)(2,1)S(1)} copy-done((bf16[1,24,1024]{2,1,0:T(8,128)(2,1)S(1)}, bf16[1,24,1024]{2,1,0:T(8,128)(2,1)}, u32[]{:S(2)}) %copy-start.2) | copy-done | bytes 49176
  4.5 0.0 copy-start.3
  4.5 0.7 %copy-done.3 = f32[48,48]{1,0:T(8,128)S(1)} copy-done((f32[48,48]{1,0:T(8,128)S(1)}, f32[48,48]{1,0:T(8,128)}, u32[]{:S(2)}) %copy-start.3) | copy-done | bytes 9240
  5.2 0.0 copy-start.4
  5.2 0.7 %copy-done.4 = f32[1,1024]{1,0:T(1,128)S(1)} copy-done((f32[1,1024]{1,0:T(1,128)S(1)}, f32[1,1024]{1,0:T(1,128)}, u32[]{:S(2)}) %copy-start.4) | copy-done | bytes 4120
  5.9 0.0 copy-start.5
  5.9 0.7 %copy-done.5 = s32[1,1024]{1,0:T(1,128)S(1)} copy-done((s32[1,1024]{1,0:T(1,128)S(1)}, s32[1,1024]{1,0:T(1,128)}, u32[]{:S(2)}) %copy-start.5) | copy-done | bytes 4120
  6.6 0.0 copy-start.6
  6.6 0.7 %copy-done.6 = s32[1,1024]{1,0:T(1,128)S(1)} copy-done((s32[1,1024]{1,0:T(1,128)S(1)}, s32[1,1024]{1,0:T(1,128)}, u32[]{:S(2)}) %copy-start.6) | copy-done | bytes 4120
  7.3 0.0 copy-start.7
  7.3 0.7 %copy-done.7 = s32[4,24]{1,0:T(4,128)S(1)} copy-done((s32[4,24]{1,0:T(4,128)S(1)}, s32[4,24]{1,0:T(4,128)}, u32[]{:S(2)}) %copy-start.7) | copy-done | bytes 408
  7.9 0.0 copy-start.8
  7.9 0.7 %copy-done.8 = s32[4]{0:T(128)S(1)} copy-done((s32[4]{0:T(128)S(1)}, s32[4]{0:T(128)}, u32[]{:S(2)}) %copy-start.8) | copy-done | bytes 40
  8.6 27.1 %shard_map.104 = (f32[16,1024]{1,0:T(8,128)S(1)}, f32[16,1024]{1,0:T(8,128)S(1)}) custom-call(f32[1,16,1024]{2,1,0:T(8,128)S(1)} %copy-done.1, f32[1,1024]{1,0:T(1,128)S(1)} %copy-done.4, bf16[1,1024,2048]{2,1,0:T(8,128)(2,1)S(1)} %copy-done, bf16[1,24,1024]{2,1,0:T(8,128)(2,1)S(1)} %copy-done.2, f32[48,48]{1,0:T(8,128)S(1)} %copy-done.3, ...), custom_call_target="tpu_custom_call" | custom-call | tf_op jit(solution)/shard_map/pallas_call | solution.py:299
  35.7 0.6 %copy.13 = f32[1,16,1024]{2,1,0:T(8,128)} copy(f32[1,16,1024]{2,1,0:T(8,128)S(1)} %bitcast.3) | data formatting | bytes 131072
  36.4 0.6 %copy.14 = f32[1,16,1024]{2,1,0:T(8,128)} copy(f32[1,16,1024]{2,1,0:T(8,128)S(1)} %bitcast.2) | data formatting | bytes 131072
Async XLA Ops:
  0.6 2.2 %copy-start = (bf16[1,1024,2048]{2,1,0:T(8,128)(2,1)S(1)}, bf16[1,1024,2048]{2,1,0:T(8,128)(2,1)}, u32[]{:S(2)}) copy-start(bf16[1,1024,2048]{2,1,0:T(8,128)(2,1)} %op.1) | copy-start | bytes 12582916
  2.8 0.8 %copy-start.1 = (f32[1,16,1024]{2,1,0:T(8,128)S(1)}, f32[1,16,1024]{2,1,0:T(8,128)}, u32[]{:S(2)}) copy-start(f32[1,16,1024]{2,1,0:T(8,128)} %loads.1) | copy-start | bytes 196612
  3.7 0.8 %copy-start.2 = (bf16[1,24,1024]{2,1,0:T(8,128)(2,1)S(1)}, bf16[1,24,1024]{2,1,0:T(8,128)(2,1)}, u32[]{:S(2)}) copy-start(bf16[1,24,1024]{2,1,0:T(8,128)(2,1)} %cm.1) | copy-start | bytes 147460
  4.5 0.7 %copy-start.3 = (f32[48,48]{1,0:T(8,128)S(1)}, f32[48,48]{1,0:T(8,128)}, u32[]{:S(2)}) copy-start(f32[48,48]{1,0:T(8,128)} %cinv.1) | copy-start | bytes 27652
  5.2 0.7 %copy-start.4 = (f32[1,1024]{1,0:T(1,128)S(1)}, f32[1,1024]{1,0:T(1,128)}, u32[]{:S(2)}) copy-start(f32[1,1024]{1,0:T(1,128)} %weights.1) | copy-start | bytes 12292
  5.9 0.7 %copy-start.5 = (s32[1,1024]{1,0:T(1,128)S(1)}, s32[1,1024]{1,0:T(1,128)}, u32[]{:S(2)}) copy-start(s32[1,1024]{1,0:T(1,128)} %lmap.1) | copy-start | bytes 12292
  6.6 0.7 %copy-start.6 = (s32[1,1024]{1,0:T(1,128)S(1)}, s32[1,1024]{1,0:T(1,128)}, u32[]{:S(2)}) copy-start(s32[1,1024]{1,0:T(1,128)} %rmap.1) | copy-start | bytes 12292
  7.3 0.7 %copy-start.7 = (s32[4,24]{1,0:T(4,128)S(1)}, s32[4,24]{1,0:T(4,128)}, u32[]{:S(2)}) copy-start(s32[4,24]{1,0:T(4,128)} %ids.1) | copy-start | bytes 1156
  7.9 0.7 %copy-start.8 = (s32[4]{0:T(128)S(1)}, s32[4]{0:T(128)}, u32[]{:S(2)}) copy-start(s32[4]{0:T(128)} %sizes.1) | copy-start | bytes 52

commit v2 on v1

--- a/solution.py
+++ b/solution.py
@@ -293,7 +293,7 @@
     W = (NC + 2 + 127) // 128 * 128
     G = S * R
     DMA = pltpu.SemaphoreType.DMA
-    anywhere = pl.BlockSpec(memory_space=pl.ANY)
+    anywhere = pl.BlockSpec(memory_space=pltpu.HBM)
     vmem = pl.BlockSpec(memory_space=pltpu.VMEM)
     out = jax.ShapeDtypeStruct((C, H), F32)
     sol, res = pl.pallas_call(
@@ -314,7 +314,7 @@
             DMA((2, R)), DMA((2, R)), DMA((2, R)), DMA((2, R)), DMA((2, G)), DMA((2, G)),
         ],
         compiler_params=pltpu.CompilerParams(
-            collective_id=0, has_side_effects=True, vmem_limit_bytes=48 * 1024 * 1024
+            collective_id=0, has_side_effects=True, vmem_limit_bytes=67_043_328
         ),
     )(loads, weights, dual_ops, corner_maps, coarse_inverse, corner_ids, iface_sizes,
       left_partner, right_partner)

time: 37.5 us -> 31.3 us (0.83)
  local copies, waits for them, and re-layouts: 9.21 us -> 2.95 us
    unnamed x20 -> x2, local copies, waits for them, and re-layouts: 9.21 us -> 2.95 us
where the time goes in v2:
time: 31.3 us; the launch traced here: 31 us
  Pallas kernels  27.4 us (88%)
  local copies, waits for them, and re-layouts  2.95 us (9%)
  between operations  0.64 us (2%)
    pallas_call x1, Pallas kernels, per_device(): pl.pallas_call(functools.partial(kernel, S, R), out_shape=(out, out), in_...  27.4 us
    unnamed x2, local copies, waits for them, and re-layouts  2.95 us

profile of v2, /device:TPU:0, one launch (start us, length us, event | category | flops | bytes accessed | tf_op | source)
XLA Modules:
  0.0 31.0 jit_solution(5196444162923319760)
XLA Ops:
  0.6 27.4 %shard_map.104 = (f32[16,1024]{1,0:T(8,128)}, f32[16,1024]{1,0:T(8,128)}) custom-call(f32[1,16,1024]{2,1,0:T(8,128)} %loads.1, f32[1,1024]{1,0:T(1,128)} %weights.1, bf16[1,1024,2048]{2,1,0:T(8,128)(2,1)} %op.1, bf16[1,24,1024]{2,1,0:T(8,128)(2,1)} %cm.1, f32[48,48]{1,0:T(8,128)} %cinv.1, s32[4,24]{1,0:T(4,128)} %ids.1, s32[4]{0:T(128)} %sizes.1, ...), custom_call_target="tpu_custom_call" | custom-call | tf_op jit(solution)/shard_map/pallas_call | solution.py:299
  28.1 1.5 %copy.13 = f32[1,16,1024]{2,1,0:T(8,128)} copy(f32[1,16,1024]{2,1,0:T(8,128)} %bitcast.3) | data formatting | bytes 131072
  29.6 1.5 %copy.14 = f32[1,16,1024]{2,1,0:T(8,128)} copy(f32[1,16,1024]{2,1,0:T(8,128)} %bitcast.2) | data formatting | bytes 131072
